TPU v7x, 8 devices: a whole 2x2x1 slice. The times are simulated.
8 devices in a mesh: dp: 1 (over z), tp: 2 (over y), ep: 4 (over x, core).
Axes of the slice: x: 2, y: 2, z: 1, core: 2. Of those that a mesh axis runs over, the one named last changes fastest.
Arguments:
- resid_in: bfloat16 [512, 2048], P(('dp', 'ep'))
- norm_scale: bfloat16 [2048], replicated
- w_router: bfloat16 [2048, 128], replicated
- w_gate: bfloat16 [128, 2048, 768], P('ep', None, 'tp')
- w_up: bfloat16 [128, 2048, 768], P('ep', None, 'tp')
- w_down: bfloat16 [128, 768, 2048], P('ep', 'tp')
- choice: int32 [512, 8], P(('dp', 'ep'))
Outputs:
- output: bfloat16 [512, 2048], P(('dp', 'ep'))
All inputs are finite; a program needn't handle non-finite values.
Results may differ from a plain program's by a relative error of at most 0.00530799.
Values are sent between devices in bfloat16 or wider.
A program may use at most 1 GiB of HBM per device.

v0:
```python
import jax
import jax.numpy as jnp
from jax import lax
from jax.sharding import PartitionSpec as P

NORM_EPS = 1e-5


def norm_route(resid_rows, norm_scale, w_router, choice_rows):
    rows_f32 = resid_rows.astype(jnp.float32)
    centered = rows_f32 - jnp.mean(rows_f32, axis=-1, keepdims=True)
    variance = jnp.mean(centered * centered, axis=-1, keepdims=True)
    normed = (centered * lax.rsqrt(variance + NORM_EPS) * norm_scale.astype(jnp.float32)).astype(jnp.bfloat16)
    logits = jnp.dot(normed, w_router, preferred_element_type=jnp.float32)
    router_probs = jax.nn.softmax(logits, axis=-1)
    expert_ids = jnp.arange(w_router.shape[1], dtype=jnp.int32)
    picked = jnp.sum(jnp.where(choice_rows[:, :, None] == expert_ids[None, None, :], router_probs[:, None, :], 0.0), axis=-1)
    gate_vals = picked / jnp.sum(picked, axis=-1, keepdims=True)
    return normed, gate_vals


def slot_table(choice_rows, experts, capacity):
    flat_ids = choice_rows.reshape(-1)
    onehot = (flat_ids[:, None] == jnp.arange(experts, dtype=jnp.int32)[None, :]).astype(jnp.int32)
    earlier = jnp.cumsum(onehot, axis=0) - onehot
    position = jnp.sum(earlier * onehot, axis=1)
    return flat_ids * capacity + position, position < capacity


def slot_sources(slot_ids, is_kept, num_slots, top_k):
    slot_match = (slot_ids[None, :] == jnp.arange(num_slots, dtype=jnp.int32)[:, None]) & is_kept[None, :]
    token_rows = jnp.arange(slot_ids.shape[0], dtype=jnp.int32) // top_k
    source_row = jnp.sum(jnp.where(slot_match, token_rows[None, :], 0), axis=1)
    return source_row, jnp.any(slot_match, axis=1)


def expert_glu(rows_in, w_gate, w_up, w_down):
    gate_act = jnp.einsum('esd,edf->esf', rows_in, w_gate, preferred_element_type=jnp.float32)
    up_act = jnp.einsum('esd,edf->esf', rows_in, w_up, preferred_element_type=jnp.float32)
    hidden = (jax.nn.silu(gate_act) * up_act).astype(jnp.bfloat16)
    return jnp.einsum('esf,efd->esd', hidden, w_down, preferred_element_type=jnp.float32).astype(jnp.bfloat16)


def solution(mesh):
    row_spec = P(('dp', 'ep'), None)

    def device_step(resid_in, norm_scale, w_router, w_gate, w_up, w_down, choice):
        tok_rows, d_model = resid_in.shape
        experts = w_router.shape[1]
        top_k = choice.shape[1]
        capacity = (2 * tok_rows * top_k + experts - 1) // experts
        normed, gate_vals = norm_route(resid_in, norm_scale, w_router, choice)
        slot_ids, is_kept = slot_table(choice, experts, capacity)
        source_row, filled = slot_sources(slot_ids, is_kept, experts * capacity, top_k)
        send_rows = jnp.where(filled[:, None], jnp.take(normed, source_row, axis=0), jnp.zeros((), jnp.bfloat16))
        send_rows = send_rows.reshape(experts, capacity, d_model)
        expert_rows = lax.all_to_all(send_rows, 'ep', 0, 1, tiled=True)
        expert_out = expert_glu(expert_rows, w_gate, w_up, w_down)
        back_rows = lax.all_to_all(expert_out, 'ep', 1, 0, tiled=True).reshape(experts * capacity, d_model)
        kept_rows = is_kept.reshape(tok_rows, top_k)
        safe_slots = jnp.where(kept_rows, slot_ids.reshape(tok_rows, top_k), 0)
        weights = jnp.where(kept_rows, gate_vals, 0.0)
        picked_rows = jnp.take(back_rows, safe_slots, axis=0)
        mixed_rows = jnp.sum(weights[:, :, None] * picked_rows, axis=1)
        tp_total = lax.psum(mixed_rows, 'tp')
        return (resid_in.astype(jnp.float32) + tp_total).astype(jnp.bfloat16)

    return jax.shard_map(device_step, mesh=mesh, in_specs=(row_spec, P(None), P(None, None), P('ep', None, 'tp'), P('ep', None, 'tp'), P('ep', 'tp', None), row_spec), out_specs=row_spec, check_vma=False)
```

profile of v0, /device:TPU:0, one launch (start us, length us, event | category | flops | bytes accessed | tf_op | source)
XLA Modules:
  0.0 388.8 jit_solution(13147566503357093286)
XLA Ops:
  6.5 0.8 copy.34
  7.4 0.1 eq.51
  7.5 0.1 eq.55
  7.6 0.1 copy.36
  7.7 0.2 fusion.10
  8.0 0.1 copy.37
  8.1 0.4 fusion.9
  8.5 1.2 convert_reduce_fusion
  9.7 1.3 fusion.4
  11.0 0.7 convert_element_type.32
  11.7 1.2 fusion.1
  12.9 1.7 select_reduce_fusion
  14.9 1.4 fusion.6
  16.3 11.0 %gather_fusion = bf16[2048,2048]{1,0:T(8,128)(2,1)} fusion(bf16[128,2048]{1,0:T(8,128)(2,1)S(1)} %fusion.6, s32[2048]{0:T(1024)S(1)} %broadcast_clamp_fusion), kind=kCustom, calls=%fused_computation | custom fusion | bytes 16785408 | tf_op jit(solution)/shard_map/jit(_take)/gather | solution.py:55
  27.3 4.6 %select_select_fusion = bf16[128,16,2048]{2,1,0:T(8,128)(2,1)S(1)} fusion(bf16[128,16,2048]{2,1,0:T(8,128)(2,1)} %bitcast.43, pred[128,16]{1,0:T(8,128)(4,1)S(1)} %compare_and_fusion, pred[128,16]{1,0:T(8,128)(4,1)S(1)} %broadcast_in_dim.89), kind=kLoop, calls=%fused_computation.3 | loop fusion | flops 8388608 | bytes 16781312 | tf_op jit(solution)/shard_map/jit(_where)/select_n | solution.py:55
  31.9 98.0 %all_to_all.33 = bf16[128,16,2048]{2,1,0:T(8,128)(2,1)} all-to-all(bf16[128,16,2048]{2,1,0:T(8,128)(2,1)S(1)} %select_select_fusion), channel_id=1, replica_groups=mesh['dp'=1,'tp'=2,'ep'=4] {'ep'}, dimensions={0} | all-to-all | bytes 16777216 | tf_op jit(solution)/shard_map/all_to_all | solution.py:57
  129.9 8.3 %copy.42 = bf16[32,4,16,2048]{3,2,1,0:T(8,128)(2,1)} copy(bf16[32,4,16,2048]{3,2,0,1:T(8,128)(2,1)} %bitcast.44) | data formatting | bytes 16777216 | tf_op jit(solution)/shard_map/all_to_all | solution.py:57
  138.2 22.9 %fusion.20 = f32[32,64,384]{2,1,0:T(8,128)} fusion(bf16[32,64,2048]{2,1,0:T(8,128)(2,1)} %bitcast.41, bf16[32,2048,384]{2,1,0:T(8,128)(2,1)} %param.10), kind=kOutput, calls=%fused_computation.59 | convolution fusion | flops 3221225472 | bytes 61865984 | tf_op jit(solution)/shard_map/esd,edf->esf/dot_general | solution.py:38
  161.0 21.9 %multiply_convert_fusion.clone.4 = bf16[32,64,384]{2,1,0:T(8,128)(2,1)S(1)} fusion(f32[32,64,384]{2,1,0:T(8,128)} %fusion.20, bf16[32,64,2048]{2,1,0:T(8,128)(2,1)} %bitcast.42, bf16[32,2048,384]{2,1,0:T(8,128)(2,1)} %param.11), kind=kOutput, calls=%fused_computation.10.clone.clone.clone.1 | convolution fusion | flops 3225944064 | bytes 63438848 | tf_op jit(solution)/shard_map/esd,edf->esf/dot_general | solution.py:39
  182.9 20.8 %convolution_convert_fusion = bf16[32,64,2048]{2,1,0:T(8,128)(2,1)} fusion(bf16[32,384,2048]{2,1,0:T(8,128)(2,1)} %param.12, bf16[32,64,384]{2,1,0:T(8,128)(2,1)S(1)} %multiply_convert_fusion.clone.4), kind=kOutput, calls=%fused_computation.8 | convolution fusion | flops 3225419776 | bytes 60293120 | tf_op jit(solution)/shard_map/esf,efd->esd/dot_general | solution.py:41
  203.7 11.2 %copy.43 = bf16[32,64,2048]{2,0,1:T(8,128)(2,1)} copy(bf16[32,64,2048]{2,1,0:T(8,128)(2,1)} %convolution_convert_fusion) | data formatting | bytes 16777216 | tf_op jit(solution)/shard_map/convert_element_type | solution.py:41
  214.9 5.8 %all-to-all-start.1 = ((bf16[32,64,2048]{2,0,1:T(8,128)(2,1)}), bf16[32,64,2048]{2,0,1:T(8,128)(2,1)}, u32[]{:S(2)}, u32[]{:S(2)}) async-start(bf16[32,64,2048]{2,0,1:T(8,128)(2,1)} %copy.43), calls=%async_computation.1 | async-start | bytes 16777216 | tf_op jit(solution)/shard_map/all_to_all | solution.py:59
  220.7 0.3 all-reduce.2.cloned.1.call-start
  221.1 0.1 copy.41
  221.4 0.4 fusion.19
  221.9 2.0 select_reduce_fusion.1
  224.0 89.5 %all-to-all-done.1 = bf16[32,64,2048]{2,0,1:T(8,128)(2,1)} async-done(((bf16[32,64,2048]{2,0,1:T(8,128)(2,1)}), bf16[32,64,2048]{2,0,1:T(8,128)(2,1)}, u32[]{:S(2)}, u32[]{:S(2)}) %all-to-all-start.1) | async-done | bytes 8388640 | tf_op jit(solution)/shard_map/all_to_all | solution.py:59
  313.5 11.4 %copy.44 = bf16[32,4,16,2048]{3,2,0,1:T(8,128)(2,1)} copy(bf16[32,4,16,2048]{3,0,2,1:T(8,128)(2,1)} %bitcast.9) | data formatting | bytes 16777216 | tf_op jit(solution)/shard_map/all_to_all | solution.py:59
  324.9 13.3 %gather_fusion.1 = bf16[1024,2048]{1,0:T(8,128)(2,1)} fusion(bf16[2048,2048]{1,0:T(8,128)(2,1)} %bitcast.40, s32[1024]{0:T(1024)S(1)} %broadcast_clamp_fusion.1), kind=kCustom, calls=%fused_computation.1 | custom fusion | bytes 8392704 | tf_op jit(solution)/shard_map/jit(_take)/gather | solution.py:63
  338.2 6.4 %multiply_reduce_fusion = f32[128,2048]{1,0:T(8,128)} fusion(bf16[1024,2048]{1,0:T(8,128)(2,1)} %gather_fusion.1, f32[128,8]{1,0:T(8,128)S(1)} %divide_select_fusion, pred[128,8]{1,0:T(8,128)(4,1)S(1)} %get-tuple-element.7), kind=kLoop, calls=%fused_computation.2 | loop fusion | flops 8126464 | bytes 5248000 | tf_op jit(solution)/shard_map/reduce_sum | solution.py:64
  344.7 35.1 %all-reduce.2.cloned.1.call-done = f32[128,2048]{1,0:T(8,128)} async-done(((f32[128,2048]{1,0:T(8,128)}), f32[128,2048]{1,0:T(8,128)}) %all-reduce.2.cloned.1.call-update) | async-done | bytes 1048592 | tf_op jit(solution)/shard_map/psum | solution.py:65
  379.8 2.1 fusion.7
  (29 shorter events, 0.8 us)
Async XLA Ops:
  6.5 214.8 %copy-start = (bf16[2048,128]{1,0:T(8,128)(2,1)S(1)}, bf16[2048,128]{1,0:T(8,128)(2,1)}, u32[]{:S(2)}) copy-start(bf16[2048,128]{1,0:T(8,128)(2,1)} %param.9) | copy-start | bytes 1572868
  214.9 6.2 %copy-start.2 = (s32[128,8]{0,1:T(8,128)S(1)}, s32[128,8]{0,1:T(8,128)}, u32[]{:S(2)}) copy-start(s32[128,8]{0,1:T(8,128)} %param.13) | copy-start | bytes 12292
  214.9 98.6 %all-to-all-start.1 = ((bf16[32,64,2048]{2,0,1:T(8,128)(2,1)}), bf16[32,64,2048]{2,0,1:T(8,128)(2,1)}, u32[]{:S(2)}, u32[]{:S(2)}) async-start(bf16[32,64,2048]{2,0,1:T(8,128)(2,1)} %copy.43), calls=%async_computation.1 | async-start | bytes 16777216 | tf_op jit(solution)/shard_map/all_to_all | solution.py:59
  220.7 159.1 %all-reduce.2.cloned.1.call-start = ((), (), s32[]{:S(2)}) async-start(), calls=%async_computation.2 | async-start | bytes 2097152 | tf_op jit(solution)/shard_map/psum | solution.py:65
  324.9 54.9 %copy-start.1 = (bf16[128,2048]{1,0:T(8,128)(2,1)S(1)}, bf16[128,2048]{1,0:T(8,128)(2,1)}, u32[]{:S(2)}) copy-start(bf16[128,2048]{1,0:T(8,128)(2,1)} %param.7) | copy-start | bytes 1572868
Sparse Core Ops, SparseCore 0:
  344.8 34.9 all-reduce.1
where the time goes:
time: 389 us
  waiting for transfers between devices  125 us (32%)
  blocking collectives  98 us (25%)
  matrix products  65.8 us (17%)
  local copies, waits for them, and re-layouts  57 us (15%)
  other arithmetic  23.6 us (6%)
  between operations  13.6 us (3%)
  starting transfers between devices  6.09 us (2%)
    all_to_all x1, blocking collectives, device_step(): expert_rows = lax.all_to_all(send_rows, 'ep', 0, 1, tiled=True)  98 us
    all_to_all x1, waiting for transfers between devices, device_step(): lax.all_to_all(expert_out, 'ep', 1, 0, tiled=True)  89.5 us
    psum x1, waiting for transfers between devices, device_step(): tp_total = lax.psum(mixed_rows, 'tp')  35.1 us
    dot_general x1, matrix products, expert_glu(): jnp.einsum('esd,edf->esf', rows_in, w_gate, preferred_element_type=jnp.fl...  22.9 us
    dot_general x1, matrix products, expert_glu(): jnp.einsum('esd,edf->esf', rows_in, w_up, preferred_element_type=jnp.floa...  21.9 us
    dot_general x1, matrix products, expert_glu(): jnp.einsum('esf,efd->esd', hidden, w_down, preferred_element_type=jnp.flo...  20.8 us
    gather x1, local copies, waits for them, and re-layouts, device_step(): picked_rows = jnp.take(back_rows, safe_slots, axis=0)  13.3 us
    all_to_all x1, local copies, waits for them, and re-layouts, device_step(): lax.all_to_all(expert_out, 'ep', 1, 0, tiled=True)  11.4 us
  transfers between devices with their start and end apart: 2, of which 2 were waited for; matrix products, arithmetic and copies ran while one was open for 1% of the time, Pallas kernels for 0%

commit v1 on v0

v1 whole, which is shorter than its diff:
```python
import functools

import jax
import jax.numpy as jnp
from jax import lax
from jax.experimental import pallas as pl
from jax.experimental.pallas import tpu as pltpu
from jax.sharding import PartitionSpec as P

NORM_EPS = 1e-5
MESH = pl.DeviceIdType.MESH
F32 = jnp.float32
BF16 = jnp.bfloat16

SLOTS = 12
HEAD_CHUNKS = 4
LAG_X = 1
LAG_Y = 3
LAG_OUT = 5


def moe_kernel(dims, x_hbm, scale_hbm, router_hbm, gate_hbm, up_hbm, down_hbm, choice_hbm, out_hbm,
               ring, xall, uall, xbatch, hid, disp, comb, qbuf, part, pair_in, row_in, col_in, out_v,
               scale_v, router_v, choice_t, ring_sem, ring_sem2, load_sem, pair_send, pair_recv, fwd_send, fwd_recv,
               hop_send, hop_recv, ch_send, ch_recv, p_send, p_recv, x_send, x_recv, y_send, y_recv, out_sem):
    tok, d_model, experts, top_k, local, width, groups, cap, cols = dims
    chunks = d_model // cols
    gate_fills, half = local, local // 2
    fills = gate_fills + 2 * chunks
    per_row = (2 * width) // cols
    ep = lax.axis_index('ep')
    tp = lax.axis_index('tp')
    dp = lax.axis_index('dp')
    sib = ep + 1 - 2 * (ep % 2)
    opp = (ep + 2) % 4
    diag = (sib + 2) % 4
    to_sib, to_opp, to_tp = (dp, tp, sib), (dp, tp, opp), (dp, 1 - tp, ep)

    def gate_copies(f, slot):
        return (pltpu.make_async_copy(gate_hbm.at[f], ring.at[slot, pl.ds(0, d_model), pl.ds(0, width)], ring_sem.at[slot]),
                pltpu.make_async_copy(up_hbm.at[f], ring.at[slot, pl.ds(0, d_model), pl.ds(width, width)], ring_sem.at[slot]))

    def down_place(i):
        return (i // per_row) * width, (i % per_row) * cols

    def start_fill(f, slot):
        @pl.when(f < gate_fills)
        def _():
            for copy in gate_copies(f, slot):
                copy.start()

        @pl.when(jnp.logical_and(f >= gate_fills, f < fills))
        def _():
            h = f - gate_fills
            c, base = h // 2, (h % 2) * half
            col = pl.multiple_of(c * cols, cols)
            for i in range(half):
                row, lane = down_place(i)
                sem = ring_sem if i < half - 1 else ring_sem2
                pltpu.make_async_copy(down_hbm.at[base + i, :, pl.ds(col, cols)],
                                      ring.at[slot, pl.ds(row, width), pl.ds(lane, cols)], sem.at[slot]).start()

    def wait_gate(slot):
        view = ring.at[slot, pl.ds(0, d_model), :]
        pltpu.make_async_copy(view, view, ring_sem.at[slot]).wait()

    def wait_down(slot):
        rows = ((half - 1) // per_row) * width
        view = ring.at[slot, pl.ds(0, rows), :]
        pltpu.make_async_copy(view, view, ring_sem.at[slot]).wait()
        row, lane = down_place(half - 1)
        view = ring.at[slot, pl.ds(row, width), pl.ds(lane, cols)]
        pltpu.make_async_copy(view, view, ring_sem2.at[slot]).wait()

    own_x = pltpu.make_async_copy(x_hbm, xall.at[ep], load_sem.at[0])
    own_choice = pltpu.make_async_copy(choice_hbm, choice_t.at[ep], load_sem.at[1])
    own_scale = pltpu.make_async_copy(scale_hbm, scale_v, load_sem.at[2])
    own_router = pltpu.make_async_copy(router_hbm, router_v, load_sem.at[3])
    own_choice.start()
    own_x.start()
    own_scale.start()

    barrier = pltpu.get_barrier_semaphore()
    for peer in (to_sib, to_opp, to_tp):
        pl.semaphore_signal(barrier, inc=1, device_id=peer, device_id_type=MESH)
    for f in range(4):
        for copy in gate_copies(f, f):
            copy.start()
    own_router.start()
    pl.semaphore_wait(barrier, 3)

    def remote(src, dst, ssem, rsem, peer):
        return pltpu.make_async_remote_copy(src_ref=src, dst_ref=dst, send_sem=ssem, recv_sem=rsem, device_id=peer, device_id_type=MESH)

    piece = tok // HEAD_CHUNKS
    to_pair = remote(x_hbm, xall.at[ep], pair_send, pair_recv, to_sib)
    hops = [remote(x_hbm.at[pl.ds(r * piece, piece), :], xall.at[ep, pl.ds(r * piece, piece), :], hop_send.at[r], hop_recv.at[r], to_opp)
            for r in range(HEAD_CHUNKS)]
    forwards = [remote(xall.at[opp, pl.ds(r * piece, piece), :], xall.at[opp, pl.ds(r * piece, piece), :], fwd_send.at[r], fwd_recv.at[r], to_sib)
                for r in range(HEAD_CHUNKS)]
    ch_pair = remote(choice_hbm, choice_t.at[ep], ch_send.at[0], ch_recv.at[0], to_sib)
    ch_hop = remote(choice_hbm, choice_t.at[ep], ch_send.at[1], ch_recv.at[1], to_opp)
    ch_fwd = remote(choice_t.at[opp], choice_t.at[opp], ch_send.at[2], ch_recv.at[2], to_sib)
    ch_hop.start()
    ch_pair.start()
    hops[0].start()
    to_pair.start()

    for r in range(1, HEAD_CHUNKS):
        hops[r].start()

    @pl.loop(4, SLOTS)
    def _(f):
        start_fill(f, f)

    row_e = lax.broadcasted_iota(jnp.int32, (experts, tok), 0)
    earlier = (lax.broadcasted_iota(jnp.int32, (tok, tok), 0) < lax.broadcasted_iota(jnp.int32, (tok, tok), 1)).astype(BF16)
    slots = local * cap
    slot_row = lax.broadcasted_iota(jnp.int32, (slots, experts), 0)
    expand_t = (lax.broadcasted_iota(jnp.int32, (slots, experts), 1) == ep * local + slot_row // cap).astype(BF16)
    slot_col = lax.broadcasted_iota(jnp.int32, (experts, slots), 1)
    expand = (lax.broadcasted_iota(jnp.int32, (experts, slots), 0) == ep * local + slot_col // cap).astype(BF16)
    cap_row = (lax.broadcasted_iota(jnp.int32, (slots, tok), 0) % cap).astype(F32)
    cap_col = (lax.broadcasted_iota(jnp.int32, (tok, slots), 1) % cap).astype(F32)

    def positions(g):
        ids = choice_t[g]
        member = jnp.zeros((experts, tok), F32)
        for k in range(top_k):
            member = jnp.where(row_e == ids[k:k + 1, :], 1.0, member)
        before = jnp.dot(member.astype(BF16), earlier, preferred_element_type=F32)
        return member, jnp.where(member > 0.0, before, 255.0)

    def dispatch_table(g):
        member, place = positions(g)
        spot = jnp.dot(expand_t, place.astype(BF16), preferred_element_type=F32)
        disp[g] = (spot == cap_row).astype(BF16)

    def combine_table(g):
        member, place = positions(g)
        logits = jnp.dot(uall[g], router_v[...], preferred_element_type=F32)
        shifted = jnp.exp(logits - jnp.max(logits, axis=-1, keepdims=True))
        probs = shifted / jnp.sum(shifted, axis=-1, keepdims=True)
        picked = jnp.where(jnp.transpose(member) > 0.0, probs, 0.0)
        gates = picked / jnp.sum(picked, axis=-1, keepdims=True)
        spot = jnp.dot(jnp.transpose(place).astype(BF16), expand, preferred_element_type=F32)
        filled = spot == cap_col
        rest = gates
        for i in range(3):
            term = rest.astype(BF16)
            rest = rest - term.astype(F32)
            wide = jnp.dot(term, expand, preferred_element_type=F32)
            comb[g, pl.ds(i * tok, tok), :] = jnp.where(filled, wide, 0.0).astype(BF16)

    def normalize(g):
        n = d_model // 128
        scale = scale_v[...].astype(F32)
        total = jnp.zeros((tok, 128), F32)
        for j in range(n):
            total = total + xall[g, :, pl.ds(j * 128, 128)].astype(F32)
        mean = jnp.sum(total, axis=-1, keepdims=True) / d_model
        square = jnp.zeros((tok, 128), F32)
        for j in range(n):
            centered = xall[g, :, pl.ds(j * 128, 128)].astype(F32) - mean
            square = square + centered * centered
        inv = lax.rsqrt(jnp.sum(square, axis=-1, keepdims=True) / d_model + NORM_EPS)
        for j in range(n):
            centered = xall[g, :, pl.ds(j * 128, 128)].astype(F32) - mean
            uall[g, :, pl.ds(j * 128, 128)] = (centered * inv * scale[j:j + 1, :]).astype(BF16)

    own_choice.wait()
    own_scale.wait()
    own_x.wait()
    dispatch_table(ep)
    normalize(ep)
    ch_pair.wait_recv()
    dispatch_table(sib)
    to_pair.wait_recv()
    normalize(sib)
    for r in range(HEAD_CHUNKS):
        hops[r].wait_recv()
        forwards[r].start()
        if r == 0:
            ch_hop.wait_recv()
            ch_fwd.start()
            dispatch_table(opp)
            ch_fwd.wait_recv()
            dispatch_table(diag)
    normalize(opp)
    for r in range(HEAD_CHUNKS):
        forwards[r].wait_recv()
    normalize(diag)
    own_router.wait()

    batch = tok // cap
    wide = 512

    @pl.loop(0, local // batch)
    def _(b):
        for g in range(groups):
            table = disp[g, pl.ds(pl.multiple_of(b * tok, tok), tok), :]
            for j in range(d_model // wide):
                xbatch[g, :, pl.ds(j * wide, wide)] = jnp.dot(table, uall[g, :, pl.ds(j * wide, wide)], preferred_element_type=F32).astype(BF16)
        combine_table(b)

        @pl.loop(0, batch)
        def _(i):
            e = b * batch + i
            slot = e % SLOTS
            wait_gate(slot)
            row = pl.multiple_of(i * cap, cap)
            rows = jnp.concatenate([xbatch[g, pl.ds(row, cap), :] for g in range(groups)], axis=0)
            both = jnp.dot(rows, ring[slot, pl.ds(0, d_model), :], preferred_element_type=F32)
            hid[e] = (jax.nn.silu(both[:, :width]) * both[:, width:]).astype(BF16)
            start_fill(e + SLOTS, slot)

    mine, theirs = ep, opp

    def pair_copy(c, j):
        return remote(part.at[c, (1 - ep % 2) + 2 * j], pair_in.at[c, j], p_send.at[c, j], p_recv.at[c, j], to_sib)

    def x_copy(c):
        return remote(part.at[c, theirs], row_in.at[c], x_send.at[c], x_recv.at[c], to_opp)

    def y_copy(c):
        return remote(part.at[c, mine], col_in.at[c], y_send.at[c], y_recv.at[c], to_tp)

    def out_copy(c):
        col = pl.multiple_of(c * cols, cols)
        return pltpu.make_async_copy(out_v.at[:, pl.ds(col, cols)], out_hbm.at[:, pl.ds(col, cols)], out_sem.at[c])

    def compute(c):
        for h in range(2):
            f = gate_fills + 2 * c + h
            slot = f % SLOTS
            wait_down(slot)
            for i in range(half):
                row, lane = down_place(i)
                e = h * half + i
                q = jnp.dot(hid[e], ring[slot, pl.ds(row, width), pl.ds(lane, cols)], preferred_element_type=F32).astype(BF16)
                for g in range(groups):
                    qbuf[g, pl.ds(e * cap, cap), :] = q[g * cap:(g + 1) * cap, :]
            start_fill(f + SLOTS, slot)
        for g in range(groups):
            terms = jnp.dot(comb[g], qbuf[g], preferred_element_type=F32)
            part[c, g] = terms[0:tok] + terms[tok:2 * tok] + terms[2 * tok:3 * tok]
        for j in range(2):
            pair_copy(c, j).start()

    def send_x(c):
        far = 1 - ep // 2
        pair_copy(c, far).wait_recv()
        part[c, theirs] = part[c, theirs] + pair_in[c, far]
        x_copy(c).start()
        pair_copy(c, 1 - far).wait_recv()
        part[c, mine] = part[c, mine] + pair_in[c, 1 - far]

    def send_y(c):
        x_copy(c).wait_recv()
        part[c, mine] = part[c, mine] + row_in[c]
        y_copy(c).start()

    def finish(c):
        y_copy(c).wait_recv()
        col = pl.multiple_of(c * cols, cols)
        total = part[c, mine] + col_in[c]
        out_v[:, pl.ds(col, cols)] = (xall[ep, :, pl.ds(col, cols)].astype(F32) + total).astype(BF16)
        out_copy(c).start()

    @pl.loop(0, chunks + LAG_OUT)
    def _(c):
        @pl.when(c < chunks)
        def _():
            compute(c)

        for lag, stage in ((LAG_X, send_x), (LAG_Y, send_y), (LAG_OUT, finish)):
            @pl.when(jnp.logical_and(c >= lag, c < chunks + lag))
            def _():
                stage(c - lag)

    to_pair.wait_send()
    for r in range(HEAD_CHUNKS):
        hops[r].wait_send()
        forwards[r].wait_send()
    ch_pair.wait_send()
    ch_hop.wait_send()
    ch_fwd.wait_send()

    @pl.loop(0, chunks)
    def _(c):
        for j in range(2):
            pair_copy(c, j).wait_send()
        x_copy(c).wait_send()
        y_copy(c).wait_send()
        out_copy(c).wait()


def solution(mesh):
    row_spec = P(('dp', 'ep'), None)

    def device_step(resid_in, norm_scale, w_router, w_gate, w_up, w_down, choice):
        tok, d_model = resid_in.shape
        experts, top_k = w_router.shape[1], choice.shape[1]
        local, width = w_gate.shape[0], w_gate.shape[2]
        groups = experts // local
        cap = (2 * tok * top_k + experts - 1) // experts
        cols = 256
        chunks = d_model // cols
        dims = (tok, d_model, experts, top_k, local, width, groups, cap, cols)
        dma = pltpu.SemaphoreType.DMA
        vmem = pltpu.VMEM
        return pl.pallas_call(
            functools.partial(moe_kernel, dims),
            out_shape=jax.ShapeDtypeStruct((tok, d_model), BF16),
            in_specs=[pl.BlockSpec(memory_space=pl.ANY)] * 7,
            out_specs=pl.BlockSpec(memory_space=pl.ANY),
            scratch_shapes=[
                vmem((SLOTS, 6 * width, 2 * width), BF16),
                vmem((groups, tok, d_model), BF16),
                vmem((groups, tok, d_model), BF16),
                vmem((groups, tok, d_model), BF16),
                vmem((local, groups * cap, width), BF16),
                vmem((groups, local * cap, tok), BF16),
                vmem((groups, 3 * tok, local * cap), BF16),
                vmem((groups, local * cap, cols), BF16),
                vmem((chunks, groups, tok, cols), F32),
                vmem((chunks, 2, tok, cols), F32),
                vmem((chunks, tok, cols), F32),
                vmem((chunks, tok, cols), F32),
                vmem((tok, d_model), BF16),
                vmem((d_model // 128, 128), BF16),
                vmem((d_model, experts), BF16),
                vmem((groups, top_k, tok), jnp.int32),
                dma((SLOTS,)), dma((SLOTS,)), dma((4,)),
                dma(()), dma(()), dma((HEAD_CHUNKS,)), dma((HEAD_CHUNKS,)), dma((HEAD_CHUNKS,)), dma((HEAD_CHUNKS,)),
                dma((3,)), dma((3,)),
                dma((chunks, 2)), dma((chunks, 2)), dma((chunks,)), dma((chunks,)), dma((chunks,)), dma((chunks,)), dma((chunks,)),
            ],
            compiler_params=pltpu.CompilerParams(collective_id=0, has_side_effects=True, vmem_limit_bytes=67043328),
        )(resid_in, norm_scale.reshape(d_model // 128, 128), w_router, w_gate, w_up, w_down, choice.T)

    return jax.shard_map(device_step, mesh=mesh, in_specs=(row_spec, P(None), P(None, None), P('ep', None, 'tp'), P('ep', None, 'tp'), P('ep', 'tp', None), row_spec), out_specs=row_spec, check_vma=False)
```

time: 389 us -> 82.1 us (0.21)
  waiting for transfers between devices: 125 us -> 0 us
  blocking collectives: 98 us -> 0 us
  Pallas kernels: 0 us -> 80.1 us
  matrix products: 65.8 us -> 0 us
  local copies, waits for them, and re-layouts: 57 us -> 1.88 us
  other arithmetic: 23.6 us -> 0 us
  between operations: 13.6 us -> 0.01 us
  starting transfers between devices: 6.09 us -> 0 us
    all_to_all x1 -> x0, blocking collectives: 98 us -> none  [device_step(): expert_rows = lax.all_to_all(send_rows, 'ep', 0, 1, tiled=True)]
    all_to_all x1 -> x0, waiting for transfers between devices: 89.5 us -> none  [device_step(): lax.all_to_all(expert_out, 'ep', 1, 0, tiled=True)]
    pallas_call x0 -> x1, Pallas kernels: none -> 80.1 us  [device_step(): pl.pallas_call(functools.partial(moe_kernel, dims), out_shape=jax.ShapeDt...]
    dot_general x4 -> x0, matrix products: 65.8 us -> none  [the longest x1 22.9 us: expert_glu(): jnp.einsum('esd,edf->esf', rows_in, w_gate, preferred_element_type=jnp.fl...]
    psum x1 -> x0, waiting for transfers between devices: 35.1 us -> none  [device_step(): tp_total = lax.psum(mixed_rows, 'tp')]
    gather x2 -> x0, local copies, waits for them, and re-layouts: 24.3 us -> none  [the longest x1 13.3 us: device_step(): picked_rows = jnp.take(back_rows, safe_slots, axis=0)]
    all_to_all x2 -> x0, local copies, waits for them, and re-layouts: 19.6 us -> none  [the longest x1 11.4 us: device_step(): lax.all_to_all(expert_out, 'ep', 1, 0, tiled=True)]
    reduce_sum x7 -> x0, other arithmetic: 13.1 us -> none  [the longest x1 6.41 us: device_step(): mixed_rows = jnp.sum(weights[:, :, None] * picked_rows, axis=1)]
  transfers between devices with their start and end apart: 2 -> 0, of which waited for: 2 -> 0; matrix products, arithmetic and copies ran while one was open for 1% -> 0% of each run, Pallas kernels for 0% -> 0%
where the time goes in v1:
time: 82.1 us; the launch traced here: 82 us
  Pallas kernels  80.1 us (98%)
  local copies, waits for them, and re-layouts  1.88 us (2%)
    pallas_call x1, Pallas kernels, device_step(): pl.pallas_call(functools.partial(moe_kernel, dims), out_shape=jax.ShapeDt...  80.1 us
    unnamed x1, local copies, waits for them, and re-layouts  1.88 us

profile of v1, /device:TPU:0, one launch (start us, length us, event | category | flops | bytes accessed | tf_op | source)
XLA Modules:
  0.0 82.0 jit_solution(10062562637772209397)
XLA Ops:
  0.0 80.1 %shard_map.73 = bf16[128,2048]{1,0:T(8,128)(2,1)} custom-call(bf16[128,2048]{1,0:T(8,128)(2,1)} %x_hbm.1, bf16[16,128]{1,0:T(8,128)(2,1)} %bitcast.2, bf16[2048,128]{1,0:T(8,128)(2,1)} %router_hbm.1, bf16[32,2048,384]{2,1,0:T(8,128)(2,1)} %gate_hbm.1, bf16[32,2048,384]{2,1,0:T(8,128)(2,1)} %up_hbm.1, bf16[32,384,2048]{2,1,0:T(8,128)(2,1)} %down_hbm.1, ...), custom_call_target="tpu_custom_call" | custom-call | tf_op jit(solution)/shard_map/pallas_call | solution.py:312
  80.1 1.9 %copy.9 = bf16[128,2048]{1,0:T(8,128)(2,1)} copy(bf16[128,2048]{1,0:T(8,128)(2,1)} %shard_map.73) | data formatting | bytes 1048576

commit v2 on v1

v2 whole, which is shorter than its diff:
```python
import functools

import jax
import jax.numpy as jnp
from jax import lax
from jax.experimental import pallas as pl
from jax.experimental.pallas import tpu as pltpu
from jax.sharding import PartitionSpec as P

NORM_EPS = 1e-5
MESH = pl.DeviceIdType.MESH
F32 = jnp.float32
BF16 = jnp.bfloat16

SLOTS = 14
PAIR_SLOTS = 4
UNROLL = 4
HEAD_CHUNKS = 4
LAG_X = 1
LAG_Y = 3
LAG_OUT = 5


def moe_kernel(dims, x_hbm, scale_hbm, router_hbm, gate_hbm, up_hbm, down_hbm, choice_hbm, out_hbm,
               ring, xall, uall, xbatch, hid, disp, comb, qbuf, part, pair_out, pair_in, row_in, col_in,
               scale_v, router_v, choice_t, ring_sem, load_sem, pair_send, pair_recv, hop_send, hop_recv, tp_send, tp_recv,
               near_send, near_recv, far_send, far_recv, ch_send, ch_recv, p_send, p_recv, x_send, x_recv, y_send, y_recv, out_sem):
    tok, d_model, experts, top_k, local, width, groups, cap, cols = dims
    chunks = d_model // cols
    half = local // 2
    fills = local + 2 * chunks
    ep = lax.axis_index('ep')
    tp = lax.axis_index('tp')
    dp = lax.axis_index('dp')
    core, side = ep % 2, ep // 2
    sib = ep + 1 - 2 * core
    opp = (ep + 2) % 4
    diag = (sib + 2) % 4
    to_sib, to_opp, to_tp = (dp, tp, sib), (dp, tp, opp), (dp, 1 - tp, ep)

    def gate_copies(f, slot):
        return (pltpu.make_async_copy(gate_hbm.at[f], ring.at[slot, :, pl.ds(0, width)], ring_sem.at[slot]),
                pltpu.make_async_copy(up_hbm.at[f], ring.at[slot, :, pl.ds(width, width)], ring_sem.at[slot]))

    def down_pieces(i):
        pieces, done = [], 0
        while done < width:
            at = i * width + done
            rows = min(width - done, d_model - at % d_model)
            pieces.append((done, rows, at % d_model, (at // d_model) * cols))
            done += rows
        return pieces

    def start_fill(f, slot):
        @pl.when(f < local)
        def _():
            for copy in gate_copies(f, slot):
                copy.start()

        @pl.when(jnp.logical_and(f >= local, f < fills))
        def _():
            h = f - local
            c, base = h // 2, (h % 2) * half
            col = pl.multiple_of(c * cols, cols)
            for i in range(half):
                for begin, rows, row, lane in down_pieces(i):
                    pltpu.make_async_copy(down_hbm.at[base + i, pl.ds(begin, rows), pl.ds(col, cols)],
                                          ring.at[slot, pl.ds(row, rows), pl.ds(lane, cols)], ring_sem.at[slot]).start()

    def wait_fill(slot):
        pltpu.make_async_copy(ring.at[slot], ring.at[slot], ring_sem.at[slot]).wait()

    own_x = pltpu.make_async_copy(x_hbm, xall.at[ep], load_sem.at[0])
    own_choice = pltpu.make_async_copy(choice_hbm, choice_t.at[ep], load_sem.at[1])
    own_scale = pltpu.make_async_copy(scale_hbm, scale_v, load_sem.at[2])
    own_router = pltpu.make_async_copy(router_hbm, router_v, load_sem.at[3])
    own_x.start()
    own_choice.start()
    own_scale.start()
    own_router.start()

    barrier = pltpu.get_barrier_semaphore()
    for peer in (to_sib, to_opp, to_tp):
        pl.semaphore_signal(barrier, inc=1, device_id=peer, device_id_type=MESH)
    for f in range(SLOTS):
        for copy in gate_copies(f, f):
            copy.start()

    def remote(src, dst, ssem, rsem, peer):
        return pltpu.make_async_remote_copy(src_ref=src, dst_ref=dst, send_sem=ssem, recv_sem=rsem, device_id=peer, device_id_type=MESH)

    mid = tok // 2
    piece = mid // HEAD_CHUNKS

    def rows_of(which, r):
        return pl.ds(pl.multiple_of(which * mid + r * piece, piece), piece)

    def same(block, rows, ssem, rsem, peer):
        return remote(xall.at[block, rows, :], xall.at[block, rows, :], ssem, rsem, peer)

    span = range(HEAD_CHUNKS)
    to_pair = remote(xall.at[ep], xall.at[ep], pair_send, pair_recv, to_sib)
    hops = [same(ep, rows_of(tp, r), hop_send.at[r], hop_recv.at[r], to_opp) for r in span]
    over = [same(opp, rows_of(tp, r), tp_send.at[r], tp_recv.at[r], to_tp) for r in span]
    near = [same(opp, rows_of(tp, r), near_send.at[r], near_recv.at[r], to_sib) for r in span]
    far = [same(opp, rows_of(1 - tp, r), far_send.at[r], far_recv.at[r], to_sib) for r in span]
    ch_pair = remote(choice_t.at[ep], choice_t.at[ep], ch_send.at[0], ch_recv.at[0], to_sib)
    ch_hop = remote(choice_t.at[ep], choice_t.at[ep], ch_send.at[1], ch_recv.at[1], to_opp)
    ch_fwd = remote(choice_t.at[opp], choice_t.at[opp], ch_send.at[2], ch_recv.at[2], to_sib)
    own_choice.wait()
    own_x.wait()
    pl.semaphore_wait(barrier, 3)
    ch_hop.start()
    for r in span:
        hops[r].start()
    ch_pair.start()
    to_pair.start()

    row_e = lax.broadcasted_iota(jnp.int32, (experts, tok), 0)
    earlier = (lax.broadcasted_iota(jnp.int32, (tok, tok), 0) < lax.broadcasted_iota(jnp.int32, (tok, tok), 1)).astype(BF16)
    slots = local * cap
    slot_row = lax.broadcasted_iota(jnp.int32, (slots, experts), 0)
    expand_t = (lax.broadcasted_iota(jnp.int32, (slots, experts), 1) == ep * local + slot_row // cap).astype(BF16)
    slot_col = lax.broadcasted_iota(jnp.int32, (experts, slots), 1)
    expand = (lax.broadcasted_iota(jnp.int32, (experts, slots), 0) == ep * local + slot_col // cap).astype(BF16)
    cap_row = (lax.broadcasted_iota(jnp.int32, (slots, tok), 0) % cap).astype(F32)
    cap_col = (lax.broadcasted_iota(jnp.int32, (tok, slots), 1) % cap).astype(F32)

    def positions(g):
        ids = choice_t[g]
        member = jnp.zeros((experts, tok), F32)
        for k in range(top_k):
            member = jnp.where(row_e == ids[k:k + 1, :], 1.0, member)
        before = jnp.dot(member.astype(BF16), earlier, preferred_element_type=F32)
        return member, jnp.where(member > 0.0, before, 255.0)

    def dispatch_table(g):
        member, place = positions(g)
        spot = jnp.dot(expand_t, place.astype(BF16), preferred_element_type=F32)
        disp[g] = (spot == cap_row).astype(BF16)

    def combine_table(g):
        member, place = positions(g)
        logits = jnp.dot(uall[g], router_v[...], preferred_element_type=F32)
        shifted = jnp.exp(logits - jnp.max(logits, axis=-1, keepdims=True))
        probs = shifted / jnp.sum(shifted, axis=-1, keepdims=True)
        picked = jnp.where(jnp.transpose(member) > 0.0, probs, 0.0)
        gates = picked / jnp.sum(picked, axis=-1, keepdims=True)
        spot = jnp.dot(jnp.transpose(place).astype(BF16), expand, preferred_element_type=F32)
        filled = spot == cap_col
        rest = gates
        for i in range(3):
            term = rest.astype(BF16)
            rest = rest - term.astype(F32)
            wide = jnp.dot(term, expand, preferred_element_type=F32)
            comb[g, pl.ds(i * tok, tok), :] = jnp.where(filled, wide, 0.0).astype(BF16)

    def normalize(g, first, rows):
        n = d_model // 128
        at = pl.ds(first, rows)
        scale = scale_v[...].astype(F32)
        total = jnp.zeros((rows, 128), F32)
        for j in range(n):
            total = total + xall[g, at, pl.ds(j * 128, 128)].astype(F32)
        mean = jnp.sum(total, axis=-1, keepdims=True) / d_model
        square = jnp.zeros((rows, 128), F32)
        for j in range(n):
            centered = xall[g, at, pl.ds(j * 128, 128)].astype(F32) - mean
            square = square + centered * centered
        inv = lax.rsqrt(jnp.sum(square, axis=-1, keepdims=True) / d_model + NORM_EPS)
        for j in range(n):
            centered = xall[g, at, pl.ds(j * 128, 128)].astype(F32) - mean
            uall[g, at, pl.ds(j * 128, 128)] = (centered * inv * scale[j:j + 1, :]).astype(BF16)

    here, there = pl.multiple_of(tp * mid, mid), pl.multiple_of((1 - tp) * mid, mid)
    own_scale.wait()
    normalize(ep, 0, tok)
    dispatch_table(ep)
    ch_pair.wait_recv()
    to_pair.wait_recv()
    normalize(sib, 0, tok)
    dispatch_table(sib)
    own_router.wait()
    combine_table(ep)

    def pass_hop(r):
        hops[r].wait_recv()
        over[r].start()
        near[r].start()

    def pass_over(r):
        over[r].wait_recv()
        far[r].start()

    ch_hop.wait_recv()
    ch_fwd.start()
    lead = 2
    for r in range(lead):
        pass_hop(r)
    combine_table(sib)
    dispatch_table(opp)
    ch_fwd.wait_recv()
    dispatch_table(diag)
    for r in range(lead, HEAD_CHUNKS):
        pass_hop(r)
        pass_over(r - lead)
    normalize(opp, here, mid)
    for r in range(HEAD_CHUNKS - lead, HEAD_CHUNKS):
        pass_over(r)
    for r in span:
        near[r].wait_recv()
    normalize(diag, here, mid)
    normalize(opp, there, mid)
    for r in span:
        far[r].wait_recv()
    normalize(diag, there, mid)

    batch = tok // cap
    wide = 512

    @pl.loop(0, local // batch)
    def _(b):
        for g in range(groups):
            table = disp[g, pl.ds(pl.multiple_of(b * tok, tok), tok), :]
            for j in range(d_model // wide):
                xbatch[g, :, pl.ds(j * wide, wide)] = jnp.dot(table, uall[g, :, pl.ds(j * wide, wide)], preferred_element_type=F32).astype(BF16)

        @pl.when(jnp.logical_and(b >= 1, b < 3))
        def _():
            combine_table(jnp.where(b == 1, opp, diag))

        @pl.loop(0, batch // UNROLL)
        def _(i):
            first = b * batch + i * UNROLL
            for k in range(UNROLL):
                wait_fill((first + k) % SLOTS)
            for k in range(UNROLL):
                row = pl.multiple_of((i * UNROLL + k) * cap, cap)
                rows = jnp.concatenate([xbatch[g, pl.ds(row, cap), :] for g in range(groups)], axis=0)
                both = jnp.dot(rows, ring[(first + k) % SLOTS], preferred_element_type=F32)
                hid[first + k] = (jax.nn.silu(both[:, :width]) * both[:, width:]).astype(BF16)
            for k in range(UNROLL):
                start_fill(first + k + SLOTS, (first + k) % SLOTS)

    def pair_copy(c, j):
        return remote(pair_out.at[c % PAIR_SLOTS, j], pair_in.at[c, j], p_send.at[c, j], p_recv.at[c, j], to_sib)

    def at_cols(c):
        return pl.ds(pl.multiple_of(c * cols, cols), cols)

    def x_copy(c):
        return remote(xbatch.at[0, :, at_cols(c)], row_in.at[:, at_cols(c)], x_send.at[c], x_recv.at[c], to_opp)

    def y_copy(c):
        return remote(xbatch.at[1, :, at_cols(c)], col_in.at[:, at_cols(c)], y_send.at[c], y_recv.at[c], to_tp)

    def out_copy(c):
        return pltpu.make_async_copy(xbatch.at[2, :, at_cols(c)], out_hbm.at[:, at_cols(c)], out_sem.at[c])

    def half_products(c, h):
        f = local + 2 * c + h
        slot = f % SLOTS
        wait_fill(slot)
        for i in range(half):
            e = h * half + i
            parts = [ring[slot, pl.ds(row, rows), pl.ds(lane, cols)] for begin, rows, row, lane in down_pieces(i)]
            weight = parts[0] if len(parts) == 1 else jnp.concatenate(parts, axis=0)
            q = jnp.dot(hid[e], weight, preferred_element_type=F32).astype(BF16)
            for g in range(groups):
                qbuf[g, pl.ds(e * cap, cap), :] = q[g * cap:(g + 1) * cap, :]
        start_fill(f + SLOTS, slot)

    def weighted(g):
        terms = jnp.dot(comb[g], qbuf[g], preferred_element_type=F32)
        return terms[0:tok] + terms[tok:2 * tok] + terms[2 * tok:3 * tok]

    def sums(c):
        @pl.when(c >= PAIR_SLOTS)
        def _():
            for j in range(2):
                pair_copy(c - PAIR_SLOTS, j).wait_send()

        for j in range(2):
            pair_out[c % PAIR_SLOTS, j] = weighted(2 * j + 1 - core)
            pair_copy(c, j).start()
        for j in range(2):
            part[c, j] = weighted(2 * j + core)

    def send_x(c):
        for j in range(2):
            pair_copy(c, j).wait_recv()
        xbatch[0, :, at_cols(c)] = (part[c, 1 - side] + pair_in[c, 1 - side]).astype(BF16)
        x_copy(c).start()
        part[c, side] = part[c, side] + pair_in[c, side]

    def send_y(c):
        x_copy(c).wait_recv()
        xbatch[1, :, at_cols(c)] = (part[c, side] + row_in[:, at_cols(c)].astype(F32)).astype(BF16)
        y_copy(c).start()

    def finish(c):
        y_copy(c).wait_recv()
        total = xbatch[1, :, at_cols(c)].astype(F32) + col_in[:, at_cols(c)].astype(F32)
        xbatch[2, :, at_cols(c)] = (xall[ep, :, at_cols(c)].astype(F32) + total).astype(BF16)
        out_copy(c).start()

    @pl.loop(0, chunks + LAG_OUT)
    def _(c):
        @pl.when(c < chunks)
        def _():
            half_products(c, 0)

        for lag, stage in ((LAG_X, send_x), (LAG_Y, send_y), (LAG_OUT, finish)):
            @pl.when(jnp.logical_and(c >= lag, c < chunks + lag))
            def _():
                stage(c - lag)

        @pl.when(c < chunks)
        def _():
            half_products(c, 1)
            sums(c)

    to_pair.wait_send()
    for copies in (hops, over, near, far):
        for r in span:
            copies[r].wait_send()
    ch_pair.wait_send()
    ch_hop.wait_send()
    ch_fwd.wait_send()

    @pl.loop(chunks - PAIR_SLOTS, chunks)
    def _(c):
        for j in range(2):
            pair_copy(c, j).wait_send()

    @pl.loop(0, chunks)
    def _(c):
        x_copy(c).wait_send()
        y_copy(c).wait_send()
        out_copy(c).wait()


def solution(mesh):
    row_spec = P(('dp', 'ep'), None)

    def device_step(resid_in, norm_scale, w_router, w_gate, w_up, w_down, choice):
        tok, d_model = resid_in.shape
        experts, top_k = w_router.shape[1], choice.shape[1]
        local, width = w_gate.shape[0], w_gate.shape[2]
        groups = experts // local
        cap = (2 * tok * top_k + experts - 1) // experts
        cols = 256
        chunks = d_model // cols
        dims = (tok, d_model, experts, top_k, local, width, groups, cap, cols)
        dma = pltpu.SemaphoreType.DMA
        vmem = pltpu.VMEM
        return pl.pallas_call(
            functools.partial(moe_kernel, dims),
            out_shape=jax.ShapeDtypeStruct((tok, d_model), BF16),
            in_specs=[pl.BlockSpec(memory_space=pl.ANY)] * 7,
            out_specs=pl.BlockSpec(memory_space=pl.ANY),
            scratch_shapes=[
                vmem((SLOTS, d_model, 2 * width), BF16),
                vmem((groups, tok, d_model), BF16),
                vmem((groups, tok, d_model), BF16),
                vmem((groups, tok, d_model), BF16),
                vmem((local, groups * cap, width), BF16),
                vmem((groups, local * cap, tok), BF16),
                vmem((groups, 3 * tok, local * cap), BF16),
                vmem((groups, local * cap, cols), BF16),
                vmem((chunks, 2, tok, cols), F32),
                vmem((PAIR_SLOTS, 2, tok, cols), F32),
                vmem((chunks, 2, tok, cols), F32),
                vmem((tok, d_model), BF16),
                vmem((tok, d_model), BF16),
                vmem((d_model // 128, 128), BF16),
                vmem((d_model, experts), BF16),
                vmem((groups, top_k, tok), jnp.int32),
                dma((SLOTS,)), dma((4,)), dma(()), dma(()),
                *[dma((HEAD_CHUNKS,)) for _ in range(8)],
                dma((3,)), dma((3,)),
                dma((chunks, 2)), dma((chunks, 2)),
                *[dma((chunks,)) for _ in range(5)],
            ],
            compiler_params=pltpu.CompilerParams(collective_id=0, has_side_effects=True, vmem_limit_bytes=67043328),
        )(resid_in, norm_scale.reshape(d_model // 128, 128), w_router, w_gate, w_up, w_down, choice.T)

    return jax.shard_map(device_step, mesh=mesh, in_specs=(row_spec, P(None), P(None, None), P('ep', None, 'tp'), P('ep', None, 'tp'), P('ep', 'tp', None), row_spec), out_specs=row_spec, check_vma=False)
```

time: 82.1 us -> 71.2 us (0.87)
  Pallas kernels: 80.1 us -> 69.2 us
    pallas_call x1, Pallas kernels: 80.1 us -> 69.2 us  [device_step(): pl.pallas_call(functools.partial(moe_kernel, dims), out_shape=jax.ShapeDt...]
where the time goes in v2:
time: 71.2 us; the launch traced here: 71.1 us
  Pallas kernels  69.2 us (97%)
  local copies, waits for them, and re-layouts  1.88 us (3%)
    pallas_call x1, Pallas kernels, device_step(): pl.pallas_call(functools.partial(moe_kernel, dims), out_shape=jax.ShapeDt...  69.2 us
    unnamed x1, local copies, waits for them, and re-layouts  1.88 us

profile of v2, /device:TPU:0, one launch (start us, length us, event | category | flops | bytes accessed | tf_op | source)
XLA Modules:
  0.0 71.1 jit_solution(5038005886548488676)
XLA Ops:
  0.0 69.2 %shard_map.73 = bf16[128,2048]{1,0:T(8,128)(2,1)} custom-call(bf16[128,2048]{1,0:T(8,128)(2,1)} %x_hbm.1, bf16[16,128]{1,0:T(8,128)(2,1)} %bitcast.2, bf16[2048,128]{1,0:T(8,128)(2,1)} %router_hbm.1, bf16[32,2048,384]{2,1,0:T(8,128)(2,1)} %gate_hbm.1, bf16[32,2048,384]{2,1,0:T(8,128)(2,1)} %up_hbm.1, bf16[32,384,2048]{2,1,0:T(8,128)(2,1)} %down_hbm.1, ...), custom_call_target="tpu_custom_call" | custom-call | tf_op jit(solution)/shard_map/pallas_call | solution.py:357
  69.2 1.9 %copy.9 = bf16[128,2048]{1,0:T(8,128)(2,1)} copy(bf16[128,2048]{1,0:T(8,128)(2,1)} %shard_map.73) | data formatting | bytes 1048576

commit v3 on v2

--- a/solution.py
+++ b/solution.py
@@ -38,34 +38,30 @@
     diag = (sib + 2) % 4
     to_sib, to_opp, to_tp = (dp, tp, sib), (dp, tp, opp), (dp, 1 - tp, ep)
 
-    def gate_copies(f, slot):
-        return (pltpu.make_async_copy(gate_hbm.at[f], ring.at[slot, :, pl.ds(0, width)], ring_sem.at[slot]),
-                pltpu.make_async_copy(up_hbm.at[f], ring.at[slot, :, pl.ds(width, width)], ring_sem.at[slot]))
-
-    def down_pieces(i):
-        pieces, done = [], 0
-        while done < width:
-            at = i * width + done
-            rows = min(width - done, d_model - at % d_model)
-            pieces.append((done, rows, at % d_model, (at // d_model) * cols))
-            done += rows
-        return pieces
+    lane_tiles = width // 128
+    row_tiles = d_model // 128
+    side_tiles = cols // 128
+    per_expert = width // 128
+
+    def start_gate(f, slot):
+        for n, source in enumerate((gate_hbm, up_hbm)):
+            for j in range(lane_tiles):
+                pltpu.make_async_copy(source.at[f, :, :, pl.ds(j * 128, 128)], ring.at[slot, n * lane_tiles + j], ring_sem.at[slot]).start()
 
     def start_fill(f, slot):
         @pl.when(f < local)
         def _():
-            for copy in gate_copies(f, slot):
-                copy.start()
+            start_gate(f, slot)
 
         @pl.when(jnp.logical_and(f >= local, f < fills))
         def _():
             h = f - local
-            c, base = h // 2, (h % 2) * half
-            col = pl.multiple_of(c * cols, cols)
-            for i in range(half):
-                for begin, rows, row, lane in down_pieces(i):
-                    pltpu.make_async_copy(down_hbm.at[base + i, pl.ds(begin, rows), pl.ds(col, cols)],
-                                          ring.at[slot, pl.ds(row, rows), pl.ds(lane, cols)], ring_sem.at[slot]).start()
+            col = (h // 2) * cols
+            base = (h % 2) * half * per_expert
+            for b in range(2 * lane_tiles):
+                lane = pl.multiple_of(col + (b // lane_tiles) * 128, 128)
+                pltpu.make_async_copy(down_hbm.at[pl.ds(base + (b % lane_tiles) * row_tiles, row_tiles), :, pl.ds(lane, 128)],
+                                      ring.at[slot, b], ring_sem.at[slot]).start()
 
     def wait_fill(slot):
         pltpu.make_async_copy(ring.at[slot], ring.at[slot], ring_sem.at[slot]).wait()
@@ -83,8 +79,7 @@
     for peer in (to_sib, to_opp, to_tp):
         pl.semaphore_signal(barrier, inc=1, device_id=peer, device_id_type=MESH)
     for f in range(SLOTS):
-        for copy in gate_copies(f, f):
-            copy.start()
+        start_gate(f, f)
 
     def remote(src, dst, ssem, rsem, peer):
         return pltpu.make_async_remote_copy(src_ref=src, dst_ref=dst, send_sem=ssem, recv_sem=rsem, device_id=peer, device_id_type=MESH)
@@ -141,7 +136,8 @@
 
     def combine_table(g):
         member, place = positions(g)
-        logits = jnp.dot(uall[g], router_v[...], preferred_element_type=F32)
+        rows = jnp.concatenate([uall[g, j] for j in range(row_tiles)], axis=1)
+        logits = jnp.dot(rows, router_v[...], preferred_element_type=F32)
         shifted = jnp.exp(logits - jnp.max(logits, axis=-1, keepdims=True))
         probs = shifted / jnp.sum(shifted, axis=-1, keepdims=True)
         picked = jnp.where(jnp.transpose(member) > 0.0, probs, 0.0)
@@ -153,7 +149,9 @@
             term = rest.astype(BF16)
             rest = rest - term.astype(F32)
             wide = jnp.dot(term, expand, preferred_element_type=F32)
-            comb[g, pl.ds(i * tok, tok), :] = jnp.where(filled, wide, 0.0).astype(BF16)
+            picked = jnp.where(filled, wide, 0.0).astype(BF16)
+            for j in range(slots // 128):
+                comb[g, j, pl.ds(i * tok, tok), :] = picked[:, j * 128:(j + 1) * 128]
 
     def normalize(g, first, rows):
         n = d_model // 128
@@ -170,7 +168,7 @@
         inv = lax.rsqrt(jnp.sum(square, axis=-1, keepdims=True) / d_model + NORM_EPS)
         for j in range(n):
             centered = xall[g, at, pl.ds(j * 128, 128)].astype(F32) - mean
-            uall[g, at, pl.ds(j * 128, 128)] = (centered * inv * scale[j:j + 1, :]).astype(BF16)
+            uall[g, j, at, :] = (centered * inv * scale[j:j + 1, :]).astype(BF16)
 
     here, there = pl.multiple_of(tp * mid, mid), pl.multiple_of((1 - tp) * mid, mid)
     own_scale.wait()
@@ -216,14 +214,17 @@
     normalize(diag, there, mid)
 
     batch = tok // cap
-    wide = 512
+    group = 4
 
     @pl.loop(0, local // batch)
     def _(b):
         for g in range(groups):
             table = disp[g, pl.ds(pl.multiple_of(b * tok, tok), tok), :]
-            for j in range(d_model // wide):
-                xbatch[g, :, pl.ds(j * wide, wide)] = jnp.dot(table, uall[g, :, pl.ds(j * wide, wide)], preferred_element_type=F32).astype(BF16)
+            for j in range(0, row_tiles, group):
+                block = jnp.concatenate([uall[g, j + t] for t in range(group)], axis=1)
+                chosen = jnp.dot(table, block, preferred_element_type=F32).astype(BF16)
+                for t in range(group):
+                    xbatch[g, j + t] = chosen[:, t * 128:(t + 1) * 128]
 
         @pl.when(jnp.logical_and(b >= 1, b < 3))
         def _():
@@ -236,9 +237,14 @@
                 wait_fill((first + k) % SLOTS)
             for k in range(UNROLL):
                 row = pl.multiple_of((i * UNROLL + k) * cap, cap)
-                rows = jnp.concatenate([xbatch[g, pl.ds(row, cap), :] for g in range(groups)], axis=0)
-                both = jnp.dot(rows, ring[(first + k) % SLOTS], preferred_element_type=F32)
-                hid[first + k] = (jax.nn.silu(both[:, :width]) * both[:, width:]).astype(BF16)
+                slot = (first + k) % SLOTS
+                rows = jnp.concatenate([jnp.concatenate([xbatch[g, j, pl.ds(row, cap), :] for g in range(groups)], axis=0)
+                                        for j in range(row_tiles)], axis=1)
+                weight = jnp.concatenate([ring[slot, j].reshape(d_model, 128) for j in range(2 * lane_tiles)], axis=1)
+                both = jnp.dot(rows, weight, preferred_element_type=F32)
+                hidden = (jax.nn.silu(both[:, :width]) * both[:, width:]).astype(BF16)
+                for j in range(lane_tiles):
+                    hid[first + k, j] = hidden[:, j * 128:(j + 1) * 128]
             for k in range(UNROLL):
                 start_fill(first + k + SLOTS, (first + k) % SLOTS)
 
@@ -248,14 +254,19 @@
     def at_cols(c):
         return pl.ds(pl.multiple_of(c * cols, cols), cols)
 
+    def at_tiles(c):
+        return pl.ds(c * side_tiles, side_tiles)
+
     def x_copy(c):
-        return remote(xbatch.at[0, :, at_cols(c)], row_in.at[:, at_cols(c)], x_send.at[c], x_recv.at[c], to_opp)
+        return remote(xbatch.at[0, at_tiles(c)], row_in.at[at_tiles(c)], x_send.at[c], x_recv.at[c], to_opp)
 
     def y_copy(c):
-        return remote(xbatch.at[1, :, at_cols(c)], col_in.at[:, at_cols(c)], y_send.at[c], y_recv.at[c], to_tp)
-
-    def out_copy(c):
-        return pltpu.make_async_copy(xbatch.at[2, :, at_cols(c)], out_hbm.at[:, at_cols(c)], out_sem.at[c])
+        return remote(xbatch.at[1, at_tiles(c)], col_in.at[at_tiles(c)], y_send.at[c], y_recv.at[c], to_tp)
+
+    def out_copies(c):
+        return [pltpu.make_async_copy(xbatch.at[2, c * side_tiles + t],
+                                      out_hbm.at[:, pl.ds(pl.multiple_of(c * cols + t * 128, 128), 128)], out_sem.at[c, t])
+                for t in range(side_tiles)]
 
     def half_products(c, h):
         f = local + 2 * c + h
@@ -263,15 +274,20 @@
         wait_fill(slot)
         for i in range(half):
             e = h * half + i
-            parts = [ring[slot, pl.ds(row, rows), pl.ds(lane, cols)] for begin, rows, row, lane in down_pieces(i)]
-            weight = parts[0] if len(parts) == 1 else jnp.concatenate(parts, axis=0)
-            q = jnp.dot(hid[e], weight, preferred_element_type=F32).astype(BF16)
+            weight = jnp.concatenate([
+                jnp.concatenate([ring[slot, a * lane_tiles + (per_expert * i + t) // row_tiles, (per_expert * i + t) % row_tiles]
+                                 for t in range(per_expert)], axis=0) for a in range(side_tiles)], axis=1)
+            hidden = jnp.concatenate([hid[e, j] for j in range(lane_tiles)], axis=1)
+            q = jnp.dot(hidden, weight, preferred_element_type=F32).astype(BF16)
             for g in range(groups):
-                qbuf[g, pl.ds(e * cap, cap), :] = q[g * cap:(g + 1) * cap, :]
+                for a in range(side_tiles):
+                    qbuf[g, a, pl.ds(e * cap, cap), :] = q[g * cap:(g + 1) * cap, a * 128:(a + 1) * 128]
         start_fill(f + SLOTS, slot)
 
     def weighted(g):
-        terms = jnp.dot(comb[g], qbuf[g], preferred_element_type=F32)
+        gates = jnp.concatenate([comb[g, j] for j in range(slots // 128)], axis=1)
+        rows = jnp.concatenate([qbuf[g, a] for a in range(side_tiles)], axis=1)
+        terms = jnp.dot(gates, rows, preferred_element_type=F32)
         return terms[0:tok] + terms[tok:2 * tok] + terms[2 * tok:3 * tok]
 
     def sums(c):
@@ -289,26 +305,35 @@
     def send_x(c):
         for j in range(2):
             pair_copy(c, j).wait_recv()
-        xbatch[0, :, at_cols(c)] = (part[c, 1 - side] + pair_in[c, 1 - side]).astype(BF16)
+        for t in range(side_tiles):
+            at = pl.ds(t * 128, 128)
+            xbatch[0, c * side_tiles + t] = (part[c, 1 - side, :, at] + pair_in[c, 1 - side, :, at]).astype(BF16)
         x_copy(c).start()
         part[c, side] = part[c, side] + pair_in[c, side]
 
     def send_y(c):
         x_copy(c).wait_recv()
-        xbatch[1, :, at_cols(c)] = (part[c, side] + row_in[:, at_cols(c)].astype(F32)).astype(BF16)
+        for t in range(side_tiles):
+            tile = c * side_tiles + t
+            xbatch[1, tile] = (part[c, side, :, pl.ds(t * 128, 128)] + row_in[tile].astype(F32)).astype(BF16)
         y_copy(c).start()
 
     def finish(c):
         y_copy(c).wait_recv()
-        total = xbatch[1, :, at_cols(c)].astype(F32) + col_in[:, at_cols(c)].astype(F32)
-        xbatch[2, :, at_cols(c)] = (xall[ep, :, at_cols(c)].astype(F32) + total).astype(BF16)
-        out_copy(c).start()
+        for t in range(side_tiles):
+            tile = c * side_tiles + t
+            total = xbatch[1, tile].astype(F32) + col_in[tile].astype(F32)
+            resid = xall[ep, :, pl.ds(pl.multiple_of(tile * 128, 128), 128)].astype(F32)
+            xbatch[2, tile] = (resid + total).astype(BF16)
+        for copy in out_copies(c):
+            copy.start()
 
     @pl.loop(0, chunks + LAG_OUT)
     def _(c):
         @pl.when(c < chunks)
         def _():
             half_products(c, 0)
+            half_products(c, 1)
 
         for lag, stage in ((LAG_X, send_x), (LAG_Y, send_y), (LAG_OUT, finish)):
             @pl.when(jnp.logical_and(c >= lag, c < chunks + lag))
@@ -317,7 +342,6 @@
 
         @pl.when(c < chunks)
         def _():
-            half_products(c, 1)
             sums(c)
 
     to_pair.wait_send()
@@ -337,7 +361,8 @@
     def _(c):
         x_copy(c).wait_send()
         y_copy(c).wait_send()
-        out_copy(c).wait()
+        for copy in out_copies(c):
+            copy.wait()
 
 
 def solution(mesh):
@@ -360,19 +385,19 @@
             in_specs=[pl.BlockSpec(memory_space=pl.ANY)] * 7,
             out_specs=pl.BlockSpec(memory_space=pl.ANY),
             scratch_shapes=[
-                vmem((SLOTS, d_model, 2 * width), BF16),
+                vmem((SLOTS, 2 * width // 128, d_model // 128, 128, 128), BF16),
                 vmem((groups, tok, d_model), BF16),
-                vmem((groups, tok, d_model), BF16),
-                vmem((groups, tok, d_model), BF16),
-                vmem((local, groups * cap, width), BF16),
+                vmem((groups, d_model // 128, tok, 128), BF16),
+                vmem((groups, d_model // 128, tok, 128), BF16),
+                vmem((local, width // 128, groups * cap, 128), BF16),
                 vmem((groups, local * cap, tok), BF16),
-                vmem((groups, 3 * tok, local * cap), BF16),
-                vmem((groups, local * cap, cols), BF16),
+                vmem((groups, local * cap // 128, 3 * tok, 128), BF16),
+                vmem((groups, cols // 128, local * cap, 128), BF16),
                 vmem((chunks, 2, tok, cols), F32),
                 vmem((PAIR_SLOTS, 2, tok, cols), F32),
                 vmem((chunks, 2, tok, cols), F32),
-                vmem((tok, d_model), BF16),
-                vmem((tok, d_model), BF16),
+                vmem((d_model // 128, tok, 128), BF16),
+                vmem((d_model // 128, tok, 128), BF16),
                 vmem((d_model // 128, 128), BF16),
                 vmem((d_model, experts), BF16),
                 vmem((groups, top_k, tok), jnp.int32),
@@ -380,9 +405,11 @@
                 *[dma((HEAD_CHUNKS,)) for _ in range(8)],
                 dma((3,)), dma((3,)),
                 dma((chunks, 2)), dma((chunks, 2)),
-                *[dma((chunks,)) for _ in range(5)],
+                *[dma((chunks,)) for _ in range(4)],
+                dma((chunks, cols // 128)),
             ],
             compiler_params=pltpu.CompilerParams(collective_id=0, has_side_effects=True, vmem_limit_bytes=67043328),
-        )(resid_in, norm_scale.reshape(d_model // 128, 128), w_router, w_gate, w_up, w_down, choice.T)
+        )(resid_in, norm_scale.reshape(d_model // 128, 128), w_router, w_gate.reshape(local, d_model // 128, 128, width),
+          w_up.reshape(local, d_model // 128, 128, width), w_down.reshape(local * width // 128, 128, d_model), choice.T)
 
     return jax.shard_map(device_step, mesh=mesh, in_specs=(row_spec, P(None), P(None, None), P('ep', None, 'tp'), P('ep', None, 'tp'), P('ep', 'tp', None), row_spec), out_specs=row_spec, check_vma=False)

time: 71.2 us -> 71.4 us (level)
  no operation moved by 1% of the time
where the time goes in v3:
time: 71.4 us; the launch traced here: 71.2 us
  Pallas kernels  69.3 us (97%)
  local copies, waits for them, and re-layouts  1.88 us (3%)
    pallas_call x1, Pallas kernels, device_step(): pl.pallas_call(functools.partial(moe_kernel, dims), out_shape=jax.ShapeDt...  69.3 us
    unnamed x1, local copies, waits for them, and re-layouts  1.88 us

profile of v3, /device:TPU:0, one launch (start us, length us, event | category | flops | bytes accessed | tf_op | source)
XLA Modules:
  0.0 71.2 jit_solution(17568627954348386201)
XLA Ops:
  0.0 69.3 %shard_map.73 = bf16[128,2048]{1,0:T(8,128)(2,1)} custom-call(bf16[128,2048]{1,0:T(8,128)(2,1)} %x_hbm.1, bf16[16,128]{1,0:T(8,128)(2,1)} %bitcast.8, bf16[2048,128]{1,0:T(8,128)(2,1)} %router_hbm.1, bf16[32,16,128,384]{3,2,1,0:T(8,128)(2,1)} %bitcast.5, bf16[32,16,128,384]{3,2,1,0:T(8,128)(2,1)} %bitcast.6, bf16[96,128,2048]{2,1,0:T(8,128)(2,1)} %bitcast.7, ...), custom_call_target="tpu_custom_call" | custom-call | tf_op jit(solution)/shard_map/pallas_call | solution.py:382
  69.3 1.9 %copy.9 = bf16[128,2048]{1,0:T(8,128)(2,1)} copy(bf16[128,2048]{1,0:T(8,128)(2,1)} %shard_map.73) | data formatting | bytes 1048576

commit v4 on v2

--- a/solution.py
+++ b/solution.py
@@ -15,7 +15,7 @@
 SLOTS = 14
 PAIR_SLOTS = 4
 UNROLL = 4
-HEAD_CHUNKS = 4
+HEAD_CHUNKS = 8
 LAG_X = 1
 LAG_Y = 3
 LAG_OUT = 5
@@ -194,7 +194,7 @@
 
     ch_hop.wait_recv()
     ch_fwd.start()
-    lead = 2
+    lead = 4
     for r in range(lead):
         pass_hop(r)
     combine_table(sib)
@@ -215,11 +215,14 @@
         far[r].wait_recv()
     normalize(diag, there, mid)
 
+    def steady(rows, weight):
+        twice = jnp.dot(jnp.concatenate([rows, rows], axis=0), weight, preferred_element_type=F32)
+        return jnp.minimum(twice[:rows.shape[0]], twice[rows.shape[0]:])
+
     batch = tok // cap
     wide = 512
 
-    @pl.loop(0, local // batch)
-    def _(b):
+    def first_products(b, refill_each):
         for g in range(groups):
             table = disp[g, pl.ds(pl.multiple_of(b * tok, tok), tok), :]
             for j in range(d_model // wide):
@@ -235,12 +238,27 @@
             for k in range(UNROLL):
                 wait_fill((first + k) % SLOTS)
             for k in range(UNROLL):
+                slot = (first + k) % SLOTS
                 row = pl.multiple_of((i * UNROLL + k) * cap, cap)
                 rows = jnp.concatenate([xbatch[g, pl.ds(row, cap), :] for g in range(groups)], axis=0)
-                both = jnp.dot(rows, ring[(first + k) % SLOTS], preferred_element_type=F32)
+                both = steady(rows, ring[slot])
+                if refill_each:
+                    for copy in gate_copies(first + k + SLOTS, slot):
+                        copy.start()
                 hid[first + k] = (jax.nn.silu(both[:, :width]) * both[:, width:]).astype(BF16)
-            for k in range(UNROLL):
-                start_fill(first + k + SLOTS, (first + k) % SLOTS)
+            if not refill_each:
+                for k in range(UNROLL):
+                    start_fill(first + k + SLOTS, (first + k) % SLOTS)
+
+    early = (local - SLOTS) // batch
+
+    @pl.loop(0, early)
+    def _(b):
+        first_products(b, True)
+
+    @pl.loop(early, local // batch)
+    def _(b):
+        first_products(b, False)
 
     def pair_copy(c, j):
         return remote(pair_out.at[c % PAIR_SLOTS, j], pair_in.at[c, j], p_send.at[c, j], p_recv.at[c, j], to_sib)
@@ -248,11 +266,16 @@
     def at_cols(c):
         return pl.ds(pl.multiple_of(c * cols, cols), cols)
 
-    def x_copy(c):
-        return remote(xbatch.at[0, :, at_cols(c)], row_in.at[:, at_cols(c)], x_send.at[c], x_recv.at[c], to_opp)
-
-    def y_copy(c):
-        return remote(xbatch.at[1, :, at_cols(c)], col_in.at[:, at_cols(c)], y_send.at[c], y_recv.at[c], to_tp)
+    halves = range(cols // 128)
+
+    def at_half(c, t):
+        return pl.ds(pl.multiple_of(c * cols + t * 128, 128), 128)
+
+    def x_copy(c, t):
+        return remote(xbatch.at[0, :, at_half(c, t)], row_in.at[c, t], x_send.at[c, t], x_recv.at[c, t], to_opp)
+
+    def y_copy(c, t):
+        return remote(xbatch.at[1, :, at_half(c, t)], col_in.at[c, t], y_send.at[c, t], y_recv.at[c, t], to_tp)
 
     def out_copy(c):
         return pltpu.make_async_copy(xbatch.at[2, :, at_cols(c)], out_hbm.at[:, at_cols(c)], out_sem.at[c])
@@ -280,28 +303,32 @@
             for j in range(2):
                 pair_copy(c - PAIR_SLOTS, j).wait_send()
 
-        for j in range(2):
+        for j in (1 - side, side):
             pair_out[c % PAIR_SLOTS, j] = weighted(2 * j + 1 - core)
             pair_copy(c, j).start()
         for j in range(2):
             part[c, j] = weighted(2 * j + core)
 
     def send_x(c):
-        for j in range(2):
-            pair_copy(c, j).wait_recv()
-        xbatch[0, :, at_cols(c)] = (part[c, 1 - side] + pair_in[c, 1 - side]).astype(BF16)
-        x_copy(c).start()
+        pair_copy(c, 1 - side).wait_recv()
+        for t in halves:
+            at = pl.ds(t * 128, 128)
+            xbatch[0, :, at_half(c, t)] = (part[c, 1 - side, :, at] + pair_in[c, 1 - side, :, at]).astype(BF16)
+            x_copy(c, t).start()
+        pair_copy(c, side).wait_recv()
         part[c, side] = part[c, side] + pair_in[c, side]
 
     def send_y(c):
-        x_copy(c).wait_recv()
-        xbatch[1, :, at_cols(c)] = (part[c, side] + row_in[:, at_cols(c)].astype(F32)).astype(BF16)
-        y_copy(c).start()
+        for t in halves:
+            x_copy(c, t).wait_recv()
+            xbatch[1, :, at_half(c, t)] = (part[c, side, :, pl.ds(t * 128, 128)] + row_in[c, t].astype(F32)).astype(BF16)
+            y_copy(c, t).start()
 
     def finish(c):
-        y_copy(c).wait_recv()
-        total = xbatch[1, :, at_cols(c)].astype(F32) + col_in[:, at_cols(c)].astype(F32)
-        xbatch[2, :, at_cols(c)] = (xall[ep, :, at_cols(c)].astype(F32) + total).astype(BF16)
+        for t in halves:
+            y_copy(c, t).wait_recv()
+            total = xbatch[1, :, at_half(c, t)].astype(F32) + col_in[c, t].astype(F32)
+            xbatch[2, :, at_half(c, t)] = (xall[ep, :, at_half(c, t)].astype(F32) + total).astype(BF16)
         out_copy(c).start()
 
     @pl.loop(0, chunks + LAG_OUT)
@@ -309,6 +336,7 @@
         @pl.when(c < chunks)
         def _():
             half_products(c, 0)
+            half_products(c, 1)
 
         for lag, stage in ((LAG_X, send_x), (LAG_Y, send_y), (LAG_OUT, finish)):
             @pl.when(jnp.logical_and(c >= lag, c < chunks + lag))
@@ -317,7 +345,6 @@
 
         @pl.when(c < chunks)
         def _():
-            half_products(c, 1)
             sums(c)
 
     to_pair.wait_send()
@@ -335,8 +362,9 @@
 
     @pl.loop(0, chunks)
     def _(c):
-        x_copy(c).wait_send()
-        y_copy(c).wait_send()
+        for t in halves:
+            x_copy(c, t).wait_send()
+            y_copy(c, t).wait_send()
         out_copy(c).wait()
 
 
@@ -371,8 +399,7 @@
                 vmem((chunks, 2, tok, cols), F32),
                 vmem((PAIR_SLOTS, 2, tok, cols), F32),
                 vmem((chunks, 2, tok, cols), F32),
-                vmem((tok, d_model), BF16),
-                vmem((tok, d_model), BF16),
+                *[vmem((chunks, cols // 128, tok, 128), BF16) for _ in range(2)],
                 vmem((d_model // 128, 128), BF16),
                 vmem((d_model, experts), BF16),
                 vmem((groups, top_k, tok), jnp.int32),
@@ -380,7 +407,8 @@
                 *[dma((HEAD_CHUNKS,)) for _ in range(8)],
                 dma((3,)), dma((3,)),
                 dma((chunks, 2)), dma((chunks, 2)),
-                *[dma((chunks,)) for _ in range(5)],
+                *[dma((chunks, cols // 128)) for _ in range(4)],
+                dma((chunks,)),
             ],
             compiler_params=pltpu.CompilerParams(collective_id=0, has_side_effects=True, vmem_limit_bytes=67043328),
         )(resid_in, norm_scale.reshape(d_model // 128, 128), w_router, w_gate, w_up, w_down, choice.T)

time: 71.2 us -> 67.7 us (0.951)
  Pallas kernels: 69.2 us -> 65.7 us
    pallas_call x1, Pallas kernels: 69.2 us -> 65.7 us  [device_step(): pl.pallas_call(functools.partial(moe_kernel, dims), out_shape=jax.ShapeDt...]
where the time goes in v4:
time: 67.7 us; the launch traced here: 67.6 us
  Pallas kernels  65.7 us (97%)
  local copies, waits for them, and re-layouts  1.88 us (3%)
    pallas_call x1, Pallas kernels, device_step(): pl.pallas_call(functools.partial(moe_kernel, dims), out_shape=jax.ShapeDt...  65.7 us
    unnamed x1, local copies, waits for them, and re-layouts  1.88 us

profile of v4, /device:TPU:0, one launch (start us, length us, event | category | flops | bytes accessed | tf_op | source)
XLA Modules:
  0.0 67.6 jit_solution(12407853878801491243)
XLA Ops:
  0.0 65.7 %shard_map.73 = bf16[128,2048]{1,0:T(8,128)(2,1)} custom-call(bf16[128,2048]{1,0:T(8,128)(2,1)} %x_hbm.1, bf16[16,128]{1,0:T(8,128)(2,1)} %bitcast.2, bf16[2048,128]{1,0:T(8,128)(2,1)} %router_hbm.1, bf16[32,2048,384]{2,1,0:T(8,128)(2,1)} %gate_hbm.1, bf16[32,2048,384]{2,1,0:T(8,128)(2,1)} %up_hbm.1, bf16[32,384,2048]{2,1,0:T(8,128)(2,1)} %down_hbm.1, ...), custom_call_target="tpu_custom_call" | custom-call | tf_op jit(solution)/shard_map/pallas_call | solution.py:385
  65.7 1.9 %copy.9 = bf16[128,2048]{1,0:T(8,128)(2,1)} copy(bf16[128,2048]{1,0:T(8,128)(2,1)} %shard_map.73) | data formatting | bytes 1048576

commit v5 on v4

--- a/solution.py
+++ b/solution.py
@@ -12,8 +12,8 @@
 F32 = jnp.float32
 BF16 = jnp.bfloat16
 
-SLOTS = 14
-PAIR_SLOTS = 4
+SLOTS = 15
+PAIR_SLOTS = 1
 UNROLL = 4
 HEAD_CHUNKS = 8
 LAG_X = 1
@@ -22,7 +22,7 @@
 
 
 def moe_kernel(dims, x_hbm, scale_hbm, router_hbm, gate_hbm, up_hbm, down_hbm, choice_hbm, out_hbm,
-               ring, xall, uall, xbatch, hid, disp, comb, qbuf, part, pair_out, pair_in, row_in, col_in,
+               ring, xall, uall, xbatch, hid, comb, qbuf, part, far_sum, pair_out, pair_in, row_in, col_in,
                scale_v, router_v, choice_t, ring_sem, load_sem, pair_send, pair_recv, hop_send, hop_recv, tp_send, tp_recv,
                near_send, near_recv, far_send, far_recv, ch_send, ch_recv, p_send, p_recv, x_send, x_recv, y_send, y_recv, out_sem):
     tok, d_model, experts, top_k, local, width, groups, cap, cols = dims
@@ -137,7 +137,7 @@
     def dispatch_table(g):
         member, place = positions(g)
         spot = jnp.dot(expand_t, place.astype(BF16), preferred_element_type=F32)
-        disp[g] = (spot == cap_row).astype(BF16)
+        qbuf[g, :, pl.ds(0, tok)] = (spot == cap_row).astype(BF16)
 
     def combine_table(g):
         member, place = positions(g)
@@ -224,7 +224,7 @@
 
     def first_products(b, refill_each):
         for g in range(groups):
-            table = disp[g, pl.ds(pl.multiple_of(b * tok, tok), tok), :]
+            table = qbuf[g, pl.ds(pl.multiple_of(b * tok, tok), tok), pl.ds(0, tok)]
             for j in range(d_model // wide):
                 xbatch[g, :, pl.ds(j * wide, wide)] = jnp.dot(table, uall[g, :, pl.ds(j * wide, wide)], preferred_element_type=F32).astype(BF16)
 
@@ -306,22 +306,22 @@
         for j in (1 - side, side):
             pair_out[c % PAIR_SLOTS, j] = weighted(2 * j + 1 - core)
             pair_copy(c, j).start()
-        for j in range(2):
-            part[c, j] = weighted(2 * j + core)
+        far_sum[...] = weighted(2 * (1 - side) + core)
+        part[c] = weighted(2 * side + core)
 
     def send_x(c):
         pair_copy(c, 1 - side).wait_recv()
         for t in halves:
             at = pl.ds(t * 128, 128)
-            xbatch[0, :, at_half(c, t)] = (part[c, 1 - side, :, at] + pair_in[c, 1 - side, :, at]).astype(BF16)
+            xbatch[0, :, at_half(c, t)] = (far_sum[:, at] + pair_in[c, 1 - side, :, at]).astype(BF16)
             x_copy(c, t).start()
         pair_copy(c, side).wait_recv()
-        part[c, side] = part[c, side] + pair_in[c, side]
+        part[c] = part[c] + pair_in[c, side]
 
     def send_y(c):
         for t in halves:
             x_copy(c, t).wait_recv()
-            xbatch[1, :, at_half(c, t)] = (part[c, side, :, pl.ds(t * 128, 128)] + row_in[c, t].astype(F32)).astype(BF16)
+            xbatch[1, :, at_half(c, t)] = (part[c, :, pl.ds(t * 128, 128)] + row_in[c, t].astype(F32)).astype(BF16)
             y_copy(c, t).start()
 
     def finish(c):
@@ -393,10 +393,10 @@
                 vmem((groups, tok, d_model), BF16),
                 vmem((groups, tok, d_model), BF16),
                 vmem((local, groups * cap, width), BF16),
-                vmem((groups, local * cap, tok), BF16),
                 vmem((groups, 3 * tok, local * cap), BF16),
                 vmem((groups, local * cap, cols), BF16),
-                vmem((chunks, 2, tok, cols), F32),
+                vmem((chunks, tok, cols), F32),
+                vmem((tok, cols), F32),
                 vmem((PAIR_SLOTS, 2, tok, cols), F32),
                 vmem((chunks, 2, tok, cols), F32),
                 *[vmem((chunks, cols // 128, tok, 128), BF16) for _ in range(2)],

time: 67.7 us -> 67.4 us (level)
  no operation moved by 1% of the time
where the time goes in v5:
time: 67.4 us; the launch traced here: 67.3 us
  Pallas kernels  65.4 us (97%)
  local copies, waits for them, and re-layouts  1.88 us (3%)
    pallas_call x1, Pallas kernels, device_step(): pl.pallas_call(functools.partial(moe_kernel, dims), out_shape=jax.ShapeDt...  65.4 us
    unnamed x1, local copies, waits for them, and re-layouts  1.88 us

profile of v5, /device:TPU:0, one launch (start us, length us, event | category | flops | bytes accessed | tf_op | source)
XLA Modules:
  0.0 67.3 jit_solution(3489633401160311465)
XLA Ops:
  0.0 65.4 %shard_map.73 = bf16[128,2048]{1,0:T(8,128)(2,1)} custom-call(bf16[128,2048]{1,0:T(8,128)(2,1)} %x_hbm.1, bf16[16,128]{1,0:T(8,128)(2,1)} %bitcast.2, bf16[2048,128]{1,0:T(8,128)(2,1)} %router_hbm.1, bf16[32,2048,384]{2,1,0:T(8,128)(2,1)} %gate_hbm.1, bf16[32,2048,384]{2,1,0:T(8,128)(2,1)} %up_hbm.1, bf16[32,384,2048]{2,1,0:T(8,128)(2,1)} %down_hbm.1, ...), custom_call_target="tpu_custom_call" | custom-call | tf_op jit(solution)/shard_map/pallas_call | solution.py:385
  65.4 1.9 %copy.9 = bf16[128,2048]{1,0:T(8,128)(2,1)} copy(bf16[128,2048]{1,0:T(8,128)(2,1)} %shard_map.73) | data formatting | bytes 1048576
